TPU v7x, 32 devices: a whole 2x2x4 slice. The times are simulated.
32 devices in a mesh: dp: 8 (over z, y), mp: 4 (over x, core).
Axes of the slice: x: 2, y: 2, z: 4, core: 2. Of those that a mesh axis runs over, the one named last changes fastest.
Arguments:
- hidden_input: bfloat16 [8192, 24], P('dp'), may hold values from -6 to 6
- output_cotangent: bfloat16 [8192, 8192], P('dp', 'mp'), may hold values from -0.023925781 to 0.023925781
- master_weights: float32 [24, 8192], P('dp', 'mp'), may hold values from -6 to 6
- first_codes: int32 [24, 8192], P('dp', 'mp'), may hold values from 0 to 15
- second_codes: int32 [24, 8192], P('dp', 'mp'), may hold values from 0 to 15
- first_rows: float32 [24], P('dp'), may hold values from 0.001 to 0.03
- first_cols: float32 [8192], P('mp'), may hold values from 0.001 to 0.03
- second_rows: float32 [24], P('dp'), may hold values from 1e-05 to 0.001
- second_cols: float32 [8192], P('mp'), may hold values from 1e-05 to 0.001
- step_count: int32 [], replicated, may hold values from 1 to 9
Outputs:
- new_master: float32 [24, 8192], P('dp', 'mp')
- update_ratio: float32 [24, 8192], P('dp', 'mp')
- gathered_params: bfloat16 [24, 8192], P(None, 'mp')
- first_scaled: float32 [24, 8192], P('dp', 'mp')
- second_scaled: float32 [24, 8192], P('dp', 'mp')
- new_first_rows: float32 [24], P('dp')
- new_first_cols: float32 [8192], P('mp')
- new_second_rows: float32 [24], P('dp')
- new_second_cols: float32 [8192], P('mp')
All inputs are finite; a program needn't handle non-finite values.
Results may differ from a plain program's by a relative error of at most 0.001.
Values may be sent and summed in bfloat16 or wider, within the bound.
A program may use at most 64 MiB of HBM per device.

v0:
```python
import functools

import jax
import jax.numpy as jnp
from jax import lax
from jax.experimental import pallas as pl
from jax.experimental.pallas import tpu as pltpu
from jax.sharding import PartitionSpec as P

MESH = pl.DeviceIdType.MESH
F32 = jnp.float32
I16 = jnp.int16
FULL = 32767.0


SUB = 8
LANES = 128


def kernel(
    ndp,
    nmp,
    loads_per_part,
    hidden_hbm,
    cot_hbm,
    master_hbm,
    code1_hbm,
    code2_hbm,
    cols1_hbm,
    cols2_hbm,
    rows1_hbm,
    rows2_hbm,
    step_hbm,
    master_out,
    ratio_out,
    params_out,
    scaled1_out,
    scaled2_out,
    rows_out,
    cols_out,
    hidden,
    cot,
    master,
    code1,
    code2,
    rows1,
    rows2,
    step_count,
    share,
    coded_share,
    share_unit,
    grads,
    grad_unit,
    packs,
    metas,
    mcodes,
    mcols,
    gq,
    gm,
    gunits,
    sums,
    gmine,
    gcoded,
    old1,
    old2,
    weights,
    all1,
    all2,
    allw,
    wide1,
    wide2,
    in_sem,
    cot_sem,
    pack_sem,
    send_sem,
    recv_sem,
):
    dp = lax.axis_index("dp")
    mp = lax.axis_index("mp")
    ndev = ndp * nmp
    flat = dp * nmp + mp
    half, side = lax.div(dp, 2), lax.rem(dp, 2)
    group, core = lax.div(mp, 2), lax.rem(mp, 2)
    lead = 2 * group + 1
    nown, quarter = ndp // 2, ndp // 4
    nsum = nmp // 2 * nown
    own = dp - quarter
    owner = (core == 1) & (own >= 0) & (own < nown)
    slot = group * nown + own
    source = core * ndp + dp
    rows, ncols = master.shape
    parts = ncols // (SUB * LANES)
    deep = rows * SUB
    high = parts * deep
    lines = parts * SUB
    pieces = parts * loads_per_part
    width = ncols // pieces

    def loop(count, body):
        def step(i, carry):
            body(i)
            return carry

        lax.fori_loop(0, count, step, 0, unroll=count <= 32)

    loads = [
        pltpu.make_async_copy(src, dst, in_sem.at[i])
        for i, (src, dst) in enumerate(
            (
                (hidden_hbm, hidden),
                (code1_hbm, code1),
                (code2_hbm, code2),
                (master_hbm, master),
                (cols1_hbm, mcols.at[mp, pl.ds(0, lines)]),
                (cols2_hbm, mcols.at[mp, pl.ds(lines, lines)]),
                (rows1_hbm, rows1),
                (rows2_hbm, rows2),
                (step_hbm, step_count),
            )
        )
    ]
    cot_loads = [
        pltpu.make_async_copy(
            cot_hbm.at[:, pl.ds(c * width, width)], cot.at[c], cot_sem.at[c]
        )
        for c in range(pieces)
    ]

    def send(src, dst, which, to):
        pltpu.make_async_remote_copy(
            src_ref=src,
            dst_ref=dst,
            send_sem=send_sem.at[which],
            recv_sem=recv_sem.at[which],
            device_id=to,
            device_id_type=MESH,
        ).start()

    def dp_peer(k):
        return {"dp": lax.rem(dp + k + 1, ndp)}

    def mp_peer(k):
        return {"mp": lax.rem(mp + k + 1, nmp)}

    barrier = pltpu.get_barrier_semaphore()

    def greet(to):
        pl.semaphore_signal(barrier, inc=1, device_id=to, device_id_type=MESH)

    loop(ndp - 1, lambda k: greet(dp_peer(k)))
    loop(ndp - 1, lambda k: greet({**dp_peer(k), "mp": mp + 1 - 2 * core}))
    loop(nmp - 1, lambda k: greet(mp_peer(k)))
    greeted = 2 * (ndp - 1) + nmp - 1

    loads[0].start()
    for copy in cot_loads + loads[1:]:
        copy.start()

    def partner(o):
        return o + jnp.where(o >= quarter, 2 * quarter, 0)

    def place(j):
        middle = (j >= quarter) & (j < quarter + nown)
        o = jnp.where(middle, j - quarter, jnp.where(j < quarter, j, j - nown))
        return o, jnp.where(middle, 0, 1)

    def to_owners(body):
        def step(k):
            o = lax.rem(dp + k, nown)

            @pl.when((core == 0) | (own != o))
            def _():
                body(o, {"dp": quarter + o, "mp": lead})

        loop(nown, step)

    def send_share(p):
        to_owners(
            lambda o, to: send(
                coded_share.at[p, o],
                grads.at[source, pl.ds(p * 2 * deep, 2 * deep)],
                0,
                to,
            )
        )

    def quantize(x):
        top = jnp.maximum(jnp.max(jnp.abs(x), axis=0, keepdims=True), 1e-30)
        code = jnp.floor(x * (FULL / top) + 0.5)
        return code.astype(jnp.int32).astype(I16), top * (1.0 / FULL)

    def code_share(p):
        def body(o):
            blocks = [
                share[p, pl.ds(pl.multiple_of(j * deep, SUB), deep), :]
                for j in (quarter + o, partner(o))
            ]
            coded, unit = quantize(jnp.concatenate(blocks, axis=0))
            coded_share[p, o] = coded
            share_unit[o, p : p + 1] = unit

        return body

    def prepare_packs():
        for copy in loads[1:]:
            copy.wait()

        def dense(value, ref):
            for b in range(ncols // LANES):
                at = (b // SUB) * deep + b % SUB
                ref[pl.ds(at, rows, stride=SUB), :] = value[:, b * LANES : (b + 1) * LANES]

        dense(code1[...].astype(F32), old1)
        dense(code2[...].astype(F32), old2)
        dense(master[...], weights)

        lane = lax.broadcasted_iota(jnp.int32, (1, LANES), 1)
        scales = jnp.zeros((1, LANES), F32)
        for r in range(rows):
            scales = jnp.where(lane == r, rows1[:, r : r + 1], scales)
            scales = jnp.where(lane == rows + r, rows2[:, r : r + 1], scales)
        coded, unit = quantize(weights[...])
        for i, plane in enumerate((old1, old2)):
            code = plane[...].astype(jnp.int32).astype(I16)
            packs[half, side, i * high : (i + 1) * high] = code
            mcodes[mp, i * high : (i + 1) * high] = code
        packs[half, side, 2 * high : 3 * high] = coded
        metas[dp, 0:1] = scales
        metas[dp, 1:2] = unit

    def send_packs():
        loop(
            ndp // 2 - 1,
            lambda k: pltpu.make_async_remote_copy(
                src_ref=packs.at[half, side],
                dst_ref=packs.at[half, side],
                send_sem=send_sem.at[2],
                recv_sem=pack_sem.at[half],
                device_id={"dp": lax.rem(dp + 2 * (k + 1), ndp)},
                device_id_type=MESH,
            ).start(),
        )
        send(packs.at[half, side], packs.at[half, side], 12, {"dp": dp + 1 - 2 * side})
        loop(ndp - 1, lambda k: send(metas.at[dp], metas.at[dp], 4, dp_peer(k)))
        loop(nmp - 1, lambda k: send(mcodes.at[mp], mcodes.at[mp], 5, mp_peer(k)))
        loop(nmp - 1, lambda k: send(mcols.at[mp], mcols.at[mp], 6, mp_peer(k)))

    loads[0].wait()
    per_piece = width // LANES
    for c in range(pieces):
        cot_loads[c].wait()
        term = jnp.dot(hidden[...], cot[c], preferred_element_type=F32)
        p = c // loads_per_part
        for i in range(per_piece):
            sub = (c % loads_per_part) * per_piece + i
            share[p, pl.ds(sub, ndp * rows, stride=SUB), :] = term[
                :, i * LANES : (i + 1) * LANES
            ]
        if c % loads_per_part == loads_per_part - 1:
            loop(nown, code_share(p))
        if c == loads_per_part - 1:
            pl.semaphore_wait(barrier, greeted)
        if c % loads_per_part == loads_per_part - 1:
            send_share(p)

    to_owners(lambda o, to: send(share_unit.at[o], grad_unit.at[source], 11, to))

    prepare_packs()
    send_packs()

    def scale(row_of, cols):
        tiles = []
        for p in range(parts):
            for r in range(rows):
                tiles.append(jnp.minimum(row_of(r), cols[p * SUB : (p + 1) * SUB]))
        return jnp.concatenate(tiles, axis=0)

    def tile(x, p, r):
        at = p * deep + r * SUB
        return x[at : at + SUB]

    def first_of(code, row_of, cols):
        return 0.9 * ((code - 7.5) / 7.5 * scale(row_of, cols))

    def second_of(code, row_of, cols):
        level = (code + 1.0) / 16.0
        return 0.95 * (level * level * scale(row_of, cols))

    def number(code):
        return code.astype(jnp.int32).astype(F32)

    cols1 = mcols[mp, 0:lines]
    cols2 = mcols[mp, lines : 2 * lines]
    moment1 = first_of(old1[...], lambda r: rows1[:, r : r + 1], cols1)
    moment2 = second_of(old2[...], lambda r: rows2[:, r : r + 1], cols2)
    steps = step_count[...].astype(F32)
    fix1 = 1.0 - jnp.exp(steps * jnp.log(F32(0.9)))
    fix2 = 1.0 - jnp.exp(steps * jnp.log(F32(0.95)))

    def wait_all(ref, count, which):
        blocks = ref.at[pl.ds(0, count)]
        pltpu.make_async_copy(blocks, blocks, which).wait()

    def at_peers(first, count, body):
        def step(k):
            for c in range(2):

                @pl.when((first + k != dp) | (core != c))
                def _(c=c):
                    body(c, {"dp": first + k, "mp": 2 * group + c})

        loop(count, step)

    def across(t, body):
        row = partner(own) if t else dp

        def step(to):
            for c in range(2):

                @pl.when((to != 2 * group + c) & ((t == 1) | (to != mp)))
                def _(c=c):
                    body(c, {"dp": row, "mp": to})

        loop(nmp, step)

    def gathers(near, far):
        at_peers(0, quarter, near)
        across(1, functools.partial(far, 1))
        at_peers(quarter, ndp - quarter, near)
        across(0, functools.partial(far, 0))

    def to_all(body):
        def step(k):
            @pl.when(k != flat)
            def _():
                body({"dp": lax.div(k, nmp), "mp": lax.rem(k, nmp)})

        loop(ndev, step)

    @pl.when(owner)
    def _():
        for p in range(parts):
            grads[source, p * 2 * deep : (p + 1) * 2 * deep] = coded_share[p, own]
        grad_unit[source] = share_unit[own]
        wait_all(grads, 2 * ndp - 1, recv_sem.at[0])
        wait_all(grad_unit, 2 * ndp - 1, recv_sem.at[11])
        lanes = jnp.zeros((1, LANES), F32)
        for c in range(2):

            def add(d, total, c=c):
                k = c * ndp + d
                sizes = [
                    jnp.broadcast_to(grad_unit[k, p : p + 1], (2 * deep, LANES))
                    for p in range(parts)
                ]
                return total + number(grads[k]) * jnp.concatenate(sizes, axis=0)

            total = jnp.zeros((2 * high, LANES), F32)
            total = lax.fori_loop(0, ndp, add, total, unroll=ndp <= 8)
            gmine[c] = total
            lanes = lanes + jnp.sum(total * total, axis=0, keepdims=True)
        sums[slot] = lanes
        to_all(lambda to: send(sums.at[slot], sums.at[slot], 1, to))
        for c in range(2):
            coded, unit = quantize(gmine[c])
            gunits[slot, c : c + 1] = unit
            for t in range(2):
                for p in range(parts):
                    at = (p * 2 + t) * deep
                    gcoded[c, t, p * deep : (p + 1) * deep] = coded[at : at + deep]
        to_all(lambda to: send(gunits.at[slot], gunits.at[slot], 8, to))
        gq[own] = gcoded[1]
        gm[mp - 1] = gcoded[0, 0]
        gathers(
            lambda c, to: send(gcoded.at[c], gq.at[own], 7, to),
            lambda t, c, to: send(gcoded.at[c, t], gm.at[2 * group + c], 9, to),
        )

    column = packs.at[:, side]
    others = column.at[pl.ds(0, ndp // 2 - 1)]
    pair = {"dp": dp + 1 - 2 * side}

    def relay():
        def forward(k):
            ahead = jnp.where(2 * half < ndp // 2, k + 1, ndp // 2 - k - 1)
            at = lax.rem(half + ahead, ndp // 2)
            block = packs.at[at, side]
            pltpu.make_async_copy(block, block, pack_sem.at[at]).wait()
            send(block, block, 3, pair)

        loop(ndp // 2 - 1, forward)

    relay()
    wait_all(metas, ndp - 1, recv_sem.at[4])
    wait_all(mcodes, nmp - 1, recv_sem.at[5])
    wait_all(mcols, nmp - 1, recv_sem.at[6])

    def prepare(j):
        meta = metas[j]
        code1 = number(packs[j // 2, j % 2, 0:high])
        code2 = number(packs[j // 2, j % 2, high : 2 * high])
        all1[j] = first_of(code1, lambda r: meta[0:1, r : r + 1], cols1)
        all2[j] = second_of(
            code2, lambda r: meta[0:1, rows + r : rows + r + 1], cols2
        )
        allw[j] = number(packs[j // 2, j % 2, 2 * high : 3 * high]) * meta[1:2]

    def prepare_wide(k):
        code1, code2 = number(mcodes[k, 0:high]), number(mcodes[k, high : 2 * high])
        wide1[k] = first_of(code1, lambda r: rows1[:, r : r + 1], mcols[k, 0:lines])
        wide2[k] = second_of(
            code2, lambda r: rows2[:, r : r + 1], mcols[k, lines : 2 * lines]
        )

    loop(nmp, prepare_wide)
    pltpu.make_async_copy(others, others, recv_sem.at[3]).wait()
    single = packs.at[half, side]
    pltpu.make_async_copy(single, single, recv_sem.at[12]).wait()
    if ndp <= 8:
        for j in range(ndp):
            prepare(j)
    else:
        lax.fori_loop(0, ndp, lambda j, c: (prepare(j), c)[1], 0)

    def settle(ref, count, which):
        @pl.when(owner)
        def _():
            wait_all(ref, count - 1, recv_sem.at[which])

        @pl.when(jnp.logical_not(owner))
        def _():
            wait_all(ref, count, recv_sem.at[which])

    settle(sums, nsum, 1)
    lanes = jnp.sum(sums[...], axis=0)
    norm = jnp.sqrt(jnp.sum(lanes, axis=1, keepdims=True))
    entries = rows * ncols * ndev
    clipf = jnp.minimum(1.0, 0.01 * jnp.sqrt(F32(entries)) / (norm + 1e-6))

    def over_rows(x):
        tops = []
        for p in range(parts):
            top = tile(x, p, 0)
            for r in range(1, rows):
                top = jnp.maximum(top, tile(x, p, r))
            tops.append(top)
        return jnp.concatenate(tops, axis=0)

    def over_cols(x):
        tops = []
        for r in range(rows):
            top = tile(x, 0, r)
            for p in range(1, parts):
                top = jnp.maximum(top, tile(x, p, r))
            tops.append(top)
        return jnp.concatenate(tops, axis=0)

    def renew(m1, m2, code, unit):
        change = number(code) * (unit * clipf)
        return m1 + 0.1 * change, m2 + 0.05 * (change * change)

    settle(gunits, nsum, 8)
    settle(gq, nown, 7)
    settle(gm, nmp - 1, 9)
    mine, which = place(dp)
    gm[mp] = gq[mine, which]

    gradient = number(gq[mine, which]) * gunits[group * nown + mine, pl.ds(core, 1)]
    clipped = clipf * gradient
    new1 = moment1 + 0.1 * clipped
    new2 = moment2 + 0.05 * (clipped * clipped)
    ratio = new1 / fix1 / (jnp.sqrt(new2 / fix2) + 1e-8)
    old_weights = weights[...]
    master_out[...] = old_weights - 0.001 * (ratio + 0.1 * old_weights)
    ratio_out[...] = ratio

    def widen(k, tops):
        unit = gunits[k // 2 * nown + mine, pl.ds(k % 2, 1)]
        now1, now2 = renew(wide1[k], wide2[k], gm[k], unit)
        return (
            jnp.maximum(tops[0], over_cols(jnp.abs(now1))),
            jnp.maximum(tops[1], over_cols(now2)),
        )

    flat_top = jnp.zeros((deep, LANES), F32)
    tops = lax.fori_loop(0, nmp, widen, (flat_top, flat_top), unroll=nmp <= 8)
    toprow = jnp.concatenate(
        [
            jnp.max(x[r * SUB : (r + 1) * SUB], axis=0, keepdims=True)
            for x in tops
            for r in range(rows)
        ],
        axis=0,
    )
    toprow = jnp.broadcast_to(jnp.max(toprow, axis=1, keepdims=True), toprow.shape)
    rows_out[...] = toprow

    def finish(j, tops):
        o, t = place(j)
        unit = gunits[group * nown + o, pl.ds(core, 1)]
        now1, now2 = renew(all1[j], all2[j], gq[o, t], unit)
        held = allw[j]
        turn = now1 / fix1 / (jnp.sqrt(now2 / fix2) + 1e-8)
        params_out[j] = (held - 0.001 * (turn + 0.1 * held)).astype(jnp.bfloat16)
        return (
            jnp.maximum(tops[0], over_rows(jnp.abs(now1))),
            jnp.maximum(tops[1], over_rows(now2)),
        )

    flat_top = jnp.zeros((lines, LANES), F32)
    top1, top2 = lax.fori_loop(0, ndp, finish, (flat_top, flat_top), unroll=ndp <= 8)
    cols_out[0] = top1
    cols_out[1] = top2
    scaled1_out[...] = new1 / (scale(lambda r: toprow[r : r + 1], top1) + 1e-8)
    scaled2_out[...] = new2 / (
        scale(lambda r: toprow[rows + r : rows + r + 1], top2) + 1e-8
    )

    def drain(ref, which):
        pltpu.make_async_copy(ref, ref, send_sem.at[which]).wait()

    for p in range(parts):
        to_owners(lambda o, to: drain(coded_share.at[p, o], 0))
    to_owners(lambda o, to: drain(share_unit.at[o], 11))

    @pl.when(owner)
    def _():
        loop(ndev - 1, lambda k: drain(sums.at[slot], 1))
        loop(ndev - 1, lambda k: drain(gunits.at[slot], 8))
        gathers(
            lambda c, to: drain(gcoded.at[c], 7),
            lambda t, c, to: drain(gcoded.at[c, t], 9),
        )

    pltpu.make_async_copy(others, others, send_sem.at[2]).wait()
    pltpu.make_async_copy(others, others, send_sem.at[3]).wait()
    pltpu.make_async_copy(single, single, send_sem.at[12]).wait()
    wait_all(metas, ndp - 1, send_sem.at[4])
    wait_all(mcodes, nmp - 1, send_sem.at[5])
    wait_all(mcols, nmp - 1, send_sem.at[6])


def unpack(
    master,
    ratio,
    params,
    scaled1,
    scaled2,
    toprows,
    topcols,
    master_out,
    ratio_out,
    params_out,
    scaled1_out,
    scaled2_out,
    rows1_out,
    cols1_out,
    rows2_out,
    cols2_out,
    wide,
):
    rows, ncols = master_out.shape
    ndp = params.shape[0]
    parts = ncols // (SUB * LANES)
    deep = rows * SUB

    cols1_out[...] = topcols[0]
    cols2_out[...] = topcols[1]
    for r in range(rows):
        rows1_out[r] = jnp.max(toprows[r : r + 1, :])
        rows2_out[r] = jnp.max(toprows[rows + r : rows + r + 1, :])
    for j in range(ndp):
        block = params[j].astype(F32)
        for p in range(parts):
            wide[p, j * deep : (j + 1) * deep] = block[p * deep : (p + 1) * deep]
    for b in range(ncols // LANES):
        p, sub = b // SUB, b % SUB
        cols = slice(b * LANES, (b + 1) * LANES)
        part = pl.ds(p * deep + sub, rows, stride=SUB)
        master_out[:, cols] = master[part, :]
        ratio_out[:, cols] = ratio[part, :]
        scaled1_out[:, cols] = scaled1[part, :]
        scaled2_out[:, cols] = scaled2[part, :]
        params_out[:, cols] = wide[p, pl.ds(sub, ndp * rows, stride=SUB), :].astype(
            jnp.bfloat16
        )


def shards(
    ndp,
    nmp,
    hidden_input,
    output_cotangent,
    master_weights,
    first_codes,
    second_codes,
    first_rows,
    first_cols,
    second_rows,
    second_cols,
    step_count,
):
    rows, ncols = master_weights.shape
    tokens, width = hidden_input.shape
    parts = ncols // (SUB * LANES)
    loads = 2
    height = parts * rows * SUB
    hbm = pl.BlockSpec(memory_space=pltpu.HBM)
    smem = pl.BlockSpec(memory_space=pltpu.SMEM)
    vmem = pl.BlockSpec(memory_space=pltpu.VMEM)
    whole = jax.ShapeDtypeStruct((rows, ncols), F32)
    block = (height, LANES)
    line = (parts * SUB, LANES)
    dense = pltpu.VMEM(block, F32)
    results = pl.pallas_call(
        functools.partial(kernel, ndp, nmp, loads),
        out_shape=(
            dense,
            dense,
            pltpu.VMEM((ndp, *block), jnp.bfloat16),
            dense,
            dense,
            pltpu.VMEM((2 * rows, LANES), F32),
            pltpu.VMEM((2, *line), F32),
        ),
        in_specs=[hbm] * 10,
        out_specs=[vmem] * 7,
        scratch_shapes=[
            pltpu.VMEM((width, tokens), jnp.bfloat16),
            pltpu.VMEM((parts * loads, tokens, ncols // (parts * loads)), jnp.bfloat16),
            pltpu.VMEM((rows, ncols), F32),
            pltpu.VMEM((rows, ncols), jnp.int32),
            pltpu.VMEM((rows, ncols), jnp.int32),
            pltpu.VMEM((1, rows), F32),
            pltpu.VMEM((1, rows), F32),
            pltpu.VMEM((1, 1), jnp.int32),
            pltpu.VMEM((parts, ndp * rows * SUB, LANES), F32),
            pltpu.VMEM((parts, ndp // 2, 2 * rows * SUB, LANES), I16),
            pltpu.VMEM((ndp // 2, parts, LANES), F32),
            pltpu.VMEM((2 * ndp, 2 * height, LANES), I16),
            pltpu.VMEM((2 * ndp, parts, LANES), F32),
            pltpu.VMEM((ndp // 2, 2, 3 * height, LANES), I16),
            pltpu.VMEM((ndp, 2, LANES), F32),
            pltpu.VMEM((nmp, 2 * height, LANES), I16),
            pltpu.VMEM((nmp, 2 * parts * SUB, LANES), F32),
            pltpu.VMEM((ndp // 2, 2, *block), I16),
            pltpu.VMEM((nmp, *block), I16),
            pltpu.VMEM((ndp * nmp // 4, 2, LANES), F32),
            pltpu.VMEM((ndp * nmp // 4, 1, LANES), F32),
            pltpu.VMEM((2, 2 * height, LANES), F32),
            pltpu.VMEM((2, 2, *block), I16),
            pltpu.VMEM(block, F32),
            pltpu.VMEM(block, F32),
            pltpu.VMEM(block, F32),
            pltpu.VMEM((ndp, *block), F32),
            pltpu.VMEM((ndp, *block), F32),
            pltpu.VMEM((ndp, *block), F32),
            pltpu.VMEM((nmp, *block), F32),
            pltpu.VMEM((nmp, *block), F32),
            pltpu.SemaphoreType.DMA((9,)),
            pltpu.SemaphoreType.DMA((parts * loads,)),
            pltpu.SemaphoreType.DMA((ndp // 2,)),
            pltpu.SemaphoreType.DMA((13,)),
            pltpu.SemaphoreType.DMA((13,)),
        ],
        compiler_params=pltpu.CompilerParams(
            collective_id=0, has_side_effects=True, vmem_limit_bytes=60 * 1024 * 1024
        ),
    )(
        hidden_input.T,
        output_cotangent,
        master_weights,
        first_codes,
        second_codes,
        first_cols.reshape(line),
        second_cols.reshape(line),
        first_rows.reshape(1, rows),
        second_rows.reshape(1, rows),
        step_count.reshape(1, 1),
    )
    scales = jax.ShapeDtypeStruct((rows,), F32)
    cols = jax.ShapeDtypeStruct(line, F32)
    outs = pl.pallas_call(
        unpack,
        out_shape=(
            whole,
            whole,
            jax.ShapeDtypeStruct((ndp * rows, ncols), jnp.bfloat16),
            whole,
            whole,
            scales,
            cols,
            scales,
            cols,
        ),
        in_specs=[vmem] * 7,
        out_specs=[vmem] * 5 + [smem, vmem] * 2,
        scratch_shapes=[pltpu.VMEM((parts, ndp * rows * SUB, LANES), F32)],
        compiler_params=pltpu.CompilerParams(vmem_limit_bytes=40 * 1024 * 1024),
    )(*results)
    return (*outs[:6], outs[6].reshape(ncols), outs[7], outs[8].reshape(ncols))


def solution(mesh):
    return jax.shard_map(
        functools.partial(shards, mesh.shape["dp"], mesh.shape["mp"]),
        mesh=mesh,
        in_specs=(
            P("dp", None),
            P("dp", "mp"),
            P("dp", "mp"),
            P("dp", "mp"),
            P("dp", "mp"),
            P("dp"),
            P("mp"),
            P("dp"),
            P("mp"),
            P(),
        ),
        out_specs=(
            P("dp", "mp"),
            P("dp", "mp"),
            P(None, "mp"),
            P("dp", "mp"),
            P("dp", "mp"),
            P("dp"),
            P("mp"),
            P("dp"),
            P("mp"),
        ),
        check_vma=False,
    )
```

profile of v0, /device:TPU:0, one launch (start us, length us, event | category | flops | bytes accessed | tf_op | source)
XLA Modules:
  0.0 19.6 jit_solution(14532874318536207787)
XLA Ops:
  1.3 17.5 %shard_map.169 = (f32[48,128]{1,0:T(8,128)S(1)}, f32[48,128]{1,0:T(8,128)S(1)}, bf16[8,48,128]{2,1,0:T(8,128)(2,1)S(1)}, f32[48,128]{1,0:T(8,128)S(1)}, f32[48,1...) custom-call(bf16[24,1024]{1,0:T(8,128)(2,1)} %bitcast.9, bf16[1024,2048]{1,0:T(8,128)(2,1)} %cot_hbm.1, ...), custom_call_target="tpu_custom_call" | custom-call | tf_op jit(solution)/shard_map/pallas_call | solution.py:615
  18.8 0.8 %shard_map.170 = (f32[3,2048]{1,0:T(4,128)}, f32[3,2048]{1,0:T(4,128)}, bf16[24,2048]{1,0:T(8,128)(2,1)}, f32[3,2048]{1,0:T(4,128)}, f32[3,2048]{1,0:T(4,128)}, ...) custom-call(f32[48,128]{1,0:T(8,128)S(1)} %get-tuple-element.25.master, ...), custom_call_target="tpu_custom_call" | custom-call | tf_op jit(solution)/shard_map/pallas_call | solution.py:683
where the time goes:
time: 19.8 us; the launch traced here: 19.6 us
  Pallas kernels  18.3 us (92%)
  between operations  1.3 us (7%)
    pallas_call x1, Pallas kernels, shards(): pl.pallas_call(functools.partial(kernel, ndp, nmp, loads), out_shape=(den...  17.5 us
    pallas_call x1, Pallas kernels, shards(): pl.pallas_call(unpack, out_shape=(whole, whole, jax.ShapeDtypeStruct((ndp...  0.76 us

commit v1 on v0

--- a/solution.py
+++ b/solution.py
@@ -71,7 +71,9 @@
     wide2,
     in_sem,
     cot_sem,
+    ready,
     pack_sem,
+    grad_sem,
     send_sem,
     recv_sem,
 ):
@@ -82,11 +84,13 @@
     half, side = lax.div(dp, 2), lax.rem(dp, 2)
     group, core = lax.div(mp, 2), lax.rem(mp, 2)
     lead = 2 * group + 1
-    nown, quarter = ndp // 2, ndp // 4
+    quarter = ndp // 4
+    nown = ndp - quarter
     nsum = nmp // 2 * nown
-    own = dp - quarter
-    owner = (core == 1) & (own >= 0) & (own < nown)
-    slot = group * nown + own
+    owner = (core == 1) & (dp < nown)
+    extra = owner & (dp >= nown - quarter)
+    slot = group * nown + dp
+    later = dp + quarter
     source = core * ndp + dp
     rows, ncols = master.shape
     parts = ncols // (SUB * LANES)
@@ -144,44 +148,74 @@
 
     barrier = pltpu.get_barrier_semaphore()
 
-    def greet(to):
-        pl.semaphore_signal(barrier, inc=1, device_id=to, device_id_type=MESH)
-
-    loop(ndp - 1, lambda k: greet(dp_peer(k)))
-    loop(ndp - 1, lambda k: greet({**dp_peer(k), "mp": mp + 1 - 2 * core}))
-    loop(nmp - 1, lambda k: greet(mp_peer(k)))
-    greeted = 2 * (ndp - 1) + nmp - 1
+    def hold(flag, count):
+        @pl.when(count > 0)
+        def _():
+            pl.semaphore_wait(flag, count)
+
+    def greet(flag, near, chosen):
+        def along(k):
+            @pl.when(chosen(k, dp))
+            def _():
+                for to in (mp, mp + 1 - 2 * core):
+                    pl.semaphore_signal(
+                        flag,
+                        inc=1,
+                        device_id={"dp": k, "mp": to},
+                        device_id_type=MESH,
+                    )
+
+        def beside(k):
+            @pl.when(chosen(k, mp))
+            def _():
+                pl.semaphore_signal(
+                    near, inc=1, device_id={"mp": k}, device_id_type=MESH
+                )
+
+        loop(ndp, along)
+        loop(nmp, beside)
+
+    above = jnp.maximum(nown - jnp.maximum(dp + 1, 0), 0)
+    greet(barrier, barrier, lambda k, me: k > me)
 
     loads[0].start()
-    for copy in cot_loads + loads[1:]:
+    for copy in loads[1:] + cot_loads:
         copy.start()
-
-    def partner(o):
-        return o + jnp.where(o >= quarter, 2 * quarter, 0)
-
-    def place(j):
-        middle = (j >= quarter) & (j < quarter + nown)
-        o = jnp.where(middle, j - quarter, jnp.where(j < quarter, j, j - nown))
-        return o, jnp.where(middle, 0, 1)
 
     def to_owners(body):
         def step(k):
-            o = lax.rem(dp + k, nown)
-
-            @pl.when((core == 0) | (own != o))
+            j = lax.rem(dp + k, ndp)
+            o = jnp.where(j < nown, j, j - quarter)
+            t = jnp.where(j < nown, 0, 1)
+
+            @pl.when((core == 0) | (dp != o))
             def _():
-                body(o, {"dp": quarter + o, "mp": lead})
-
-        loop(nown, step)
+                body(j, t, {"dp": o, "mp": lead})
+
+        loop(ndp, step)
 
     def send_share(p):
         to_owners(
-            lambda o, to: send(
-                coded_share.at[p, o],
-                grads.at[source, pl.ds(p * 2 * deep, 2 * deep)],
-                0,
-                to,
-            )
+            lambda j, t, to: pltpu.make_async_remote_copy(
+                src_ref=coded_share.at[p, j],
+                dst_ref=grads.at[t, source, pl.ds(p * deep, deep)],
+                send_sem=send_sem.at[0],
+                recv_sem=grad_sem.at[t],
+                device_id=to,
+                device_id_type=MESH,
+            ).start()
+        )
+
+    def send_units():
+        to_owners(
+            lambda j, t, to: pltpu.make_async_remote_copy(
+                src_ref=share_unit.at[j],
+                dst_ref=grad_unit.at[t, source],
+                send_sem=send_sem.at[11],
+                recv_sem=grad_sem.at[2 + t],
+                device_id=to,
+                device_id_type=MESH,
+            ).start()
         )
 
     def quantize(x):
@@ -190,14 +224,11 @@
         return code.astype(jnp.int32).astype(I16), top * (1.0 / FULL)
 
     def code_share(p):
-        def body(o):
-            blocks = [
-                share[p, pl.ds(pl.multiple_of(j * deep, SUB), deep), :]
-                for j in (quarter + o, partner(o))
-            ]
-            coded, unit = quantize(jnp.concatenate(blocks, axis=0))
-            coded_share[p, o] = coded
-            share_unit[o, p : p + 1] = unit
+        def body(j):
+            block = pl.ds(pl.multiple_of(j * deep, SUB), deep)
+            coded, unit = quantize(share[p, block, :])
+            coded_share[p, j] = coded
+            share_unit[j, p : p + 1] = unit
 
         return body
 
@@ -228,22 +259,47 @@
         metas[dp, 0:1] = scales
         metas[dp, 1:2] = unit
 
+    def early(to):
+        return (to < half) & ((half < ndp // 2 - 1) | (to == 0))
+
+    def send_pack(to):
+        pltpu.make_async_remote_copy(
+            src_ref=packs.at[half, side],
+            dst_ref=packs.at[half, side],
+            send_sem=send_sem.at[2],
+            recv_sem=pack_sem.at[half],
+            device_id={"dp": 2 * to + side},
+            device_id_type=MESH,
+        ).start()
+
+    def send_single():
+        block = packs.at[half, side]
+        send(block, block, 12, {"dp": dp + 1 - 2 * side})
+
     def send_packs():
-        loop(
-            ndp // 2 - 1,
-            lambda k: pltpu.make_async_remote_copy(
-                src_ref=packs.at[half, side],
-                dst_ref=packs.at[half, side],
-                send_sem=send_sem.at[2],
-                recv_sem=pack_sem.at[half],
-                device_id={"dp": lax.rem(dp + 2 * (k + 1), ndp)},
-                device_id_type=MESH,
-            ).start(),
-        )
-        send(packs.at[half, side], packs.at[half, side], 12, {"dp": dp + 1 - 2 * side})
+        def rest(to):
+            @pl.when((to != half) & jnp.logical_not(early(to)))
+            def _():
+                send_pack(to)
+
+        loop(ndp // 2, rest)
+
+        send_single()
         loop(ndp - 1, lambda k: send(metas.at[dp], metas.at[dp], 4, dp_peer(k)))
         loop(nmp - 1, lambda k: send(mcodes.at[mp], mcodes.at[mp], 5, mp_peer(k)))
         loop(nmp - 1, lambda k: send(mcols.at[mp], mcols.at[mp], 6, mp_peer(k)))
+
+    hold(barrier, 2 * dp + mp)
+    which = jnp.where(owner, 0, 1)
+    greet(ready.at[which], ready.at[0], lambda k, me: k < me)
+    prepare_packs()
+
+    def ahead(to):
+        @pl.when(early(to))
+        def _():
+            send_pack(to)
+
+    loop(ndp // 2, ahead)
 
     loads[0].wait()
     per_piece = width // LANES
@@ -257,15 +313,15 @@
                 :, i * LANES : (i + 1) * LANES
             ]
         if c % loads_per_part == loads_per_part - 1:
-            loop(nown, code_share(p))
+            loop(ndp, code_share(p))
         if c == loads_per_part - 1:
-            pl.semaphore_wait(barrier, greeted)
+            hold(ready.at[0], above + nmp - 1 - mp)
         if c % loads_per_part == loads_per_part - 1:
             send_share(p)
 
-    to_owners(lambda o, to: send(share_unit.at[o], grad_unit.at[source], 11, to))
-
-    prepare_packs()
+    send_units()
+    hold(ready.at[1], 2 * (ndp - 1 - dp) - above)
+
     send_packs()
 
     def scale(row_of, cols):
@@ -312,7 +368,7 @@
         loop(count, step)
 
     def across(t, body):
-        row = partner(own) if t else dp
+        row = later if t else dp
 
         def step(to):
             for c in range(2):
@@ -322,12 +378,6 @@
                     body(c, {"dp": row, "mp": to})
 
         loop(nmp, step)
-
-    def gathers(near, far):
-        at_peers(0, quarter, near)
-        across(1, functools.partial(far, 1))
-        at_peers(quarter, ndp - quarter, near)
-        across(0, functools.partial(far, 0))
 
     def to_all(body):
         def step(k):
@@ -337,44 +387,69 @@
 
         loop(ndev, step)
 
-    @pl.when(owner)
-    def _():
+    def collect(t):
+        j = later if t else dp
         for p in range(parts):
-            grads[source, p * 2 * deep : (p + 1) * 2 * deep] = coded_share[p, own]
-        grad_unit[source] = share_unit[own]
-        wait_all(grads, 2 * ndp - 1, recv_sem.at[0])
-        wait_all(grad_unit, 2 * ndp - 1, recv_sem.at[11])
+            grads[t, source, p * deep : (p + 1) * deep] = coded_share[p, j]
+        grad_unit[t, source] = share_unit[j]
+        rest = grads.at[t, pl.ds(0, 2 * ndp - 1)]
+        pltpu.make_async_copy(rest, rest, grad_sem.at[t]).wait()
+        rest = grad_unit.at[t, pl.ds(0, 2 * ndp - 1)]
+        pltpu.make_async_copy(rest, rest, grad_sem.at[2 + t]).wait()
         lanes = jnp.zeros((1, LANES), F32)
         for c in range(2):
 
             def add(d, total, c=c):
                 k = c * ndp + d
                 sizes = [
-                    jnp.broadcast_to(grad_unit[k, p : p + 1], (2 * deep, LANES))
+                    jnp.broadcast_to(grad_unit[t, k, p : p + 1], (deep, LANES))
                     for p in range(parts)
                 ]
-                return total + number(grads[k]) * jnp.concatenate(sizes, axis=0)
-
-            total = jnp.zeros((2 * high, LANES), F32)
+                return total + number(grads[t, k]) * jnp.concatenate(sizes, axis=0)
+
+            total = jnp.zeros((high, LANES), F32)
             total = lax.fori_loop(0, ndp, add, total, unroll=ndp <= 8)
-            gmine[c] = total
+            gmine[t, c] = total
             lanes = lanes + jnp.sum(total * total, axis=0, keepdims=True)
-        sums[slot] = lanes
+        return lanes
+
+    def code_sum(t):
+        j = later if t else dp
+        for c in range(2):
+            coded, unit = quantize(gmine[t, c])
+            gunits[group * ndp + j, c : c + 1] = unit
+            gcoded[t, c] = coded
+        gq[j] = gcoded[t, 1]
+
+    def send_sum(t):
+        j = later if t else dp
+        units = gunits.at[group * ndp + j]
+        to_all(lambda to: send(units, units, 8, to))
+        at_peers(0, quarter, lambda c, to: send(gcoded.at[t, c], gq.at[j], 7, to))
+        across(t, lambda c, to: send(gcoded.at[t, c], gm.at[2 * group + c], 9, to))
+        at_peers(
+            quarter,
+            ndp - quarter,
+            lambda c, to: send(gcoded.at[t, c], gq.at[j], 7, to),
+        )
+
+    @pl.when(owner)
+    def _():
+        sums[slot] = collect(0)
+
+        @pl.when(extra)
+        def _():
+            sums[slot] = sums[slot] + collect(1)
+
         to_all(lambda to: send(sums.at[slot], sums.at[slot], 1, to))
-        for c in range(2):
-            coded, unit = quantize(gmine[c])
-            gunits[slot, c : c + 1] = unit
-            for t in range(2):
-                for p in range(parts):
-                    at = (p * 2 + t) * deep
-                    gcoded[c, t, p * deep : (p + 1) * deep] = coded[at : at + deep]
-        to_all(lambda to: send(gunits.at[slot], gunits.at[slot], 8, to))
-        gq[own] = gcoded[1]
+        code_sum(0)
         gm[mp - 1] = gcoded[0, 0]
-        gathers(
-            lambda c, to: send(gcoded.at[c], gq.at[own], 7, to),
-            lambda t, c, to: send(gcoded.at[c, t], gm.at[2 * group + c], 9, to),
-        )
+        send_sum(0)
+
+        @pl.when(extra)
+        def _():
+            code_sum(1)
+            send_sum(1)
 
     column = packs.at[:, side]
     others = column.at[pl.ds(0, ndp // 2 - 1)]
@@ -422,16 +497,20 @@
     else:
         lax.fori_loop(0, ndp, lambda j, c: (prepare(j), c)[1], 0)
 
-    def settle(ref, count, which):
-        @pl.when(owner)
-        def _():
-            wait_all(ref, count - 1, recv_sem.at[which])
-
+    def settle(ref, count, which, two):
         @pl.when(jnp.logical_not(owner))
         def _():
             wait_all(ref, count, recv_sem.at[which])
 
-    settle(sums, nsum, 1)
+        @pl.when(owner & jnp.logical_not(extra))
+        def _():
+            wait_all(ref, count - 1, recv_sem.at[which])
+
+        @pl.when(extra)
+        def _():
+            wait_all(ref, count - two, recv_sem.at[which])
+
+    settle(sums, nsum, 1, 1)
     lanes = jnp.sum(sums[...], axis=0)
     norm = jnp.sqrt(jnp.sum(lanes, axis=1, keepdims=True))
     entries = rows * ncols * ndev
@@ -459,13 +538,12 @@
         change = number(code) * (unit * clipf)
         return m1 + 0.1 * change, m2 + 0.05 * (change * change)
 
-    settle(gunits, nsum, 8)
-    settle(gq, nown, 7)
-    settle(gm, nmp - 1, 9)
-    mine, which = place(dp)
-    gm[mp] = gq[mine, which]
-
-    gradient = number(gq[mine, which]) * gunits[group * nown + mine, pl.ds(core, 1)]
+    settle(gunits, nmp // 2 * ndp, 8, 2)
+    settle(gq, ndp, 7, 2)
+    settle(gm, nmp - 1, 9, 1)
+    gm[mp] = gq[dp]
+
+    gradient = number(gq[dp]) * gunits[group * ndp + dp, pl.ds(core, 1)]
     clipped = clipf * gradient
     new1 = moment1 + 0.1 * clipped
     new2 = moment2 + 0.05 * (clipped * clipped)
@@ -475,7 +553,7 @@
     ratio_out[...] = ratio
 
     def widen(k, tops):
-        unit = gunits[k // 2 * nown + mine, pl.ds(k % 2, 1)]
+        unit = gunits[k // 2 * ndp + dp, pl.ds(k % 2, 1)]
         now1, now2 = renew(wide1[k], wide2[k], gm[k], unit)
         return (
             jnp.maximum(tops[0], over_cols(jnp.abs(now1))),
@@ -496,9 +574,8 @@
     rows_out[...] = toprow
 
     def finish(j, tops):
-        o, t = place(j)
-        unit = gunits[group * nown + o, pl.ds(core, 1)]
-        now1, now2 = renew(all1[j], all2[j], gq[o, t], unit)
+        unit = gunits[group * ndp + j, pl.ds(core, 1)]
+        now1, now2 = renew(all1[j], all2[j], gq[j], unit)
         held = allw[j]
         turn = now1 / fix1 / (jnp.sqrt(now2 / fix2) + 1e-8)
         params_out[j] = (held - 0.001 * (turn + 0.1 * held)).astype(jnp.bfloat16)
@@ -520,17 +597,22 @@
         pltpu.make_async_copy(ref, ref, send_sem.at[which]).wait()
 
     for p in range(parts):
-        to_owners(lambda o, to: drain(coded_share.at[p, o], 0))
-    to_owners(lambda o, to: drain(share_unit.at[o], 11))
+        to_owners(lambda j, t, to: drain(coded_share.at[p, j], 0))
+    to_owners(lambda j, t, to: drain(share_unit.at[j], 11))
+
+    def drain_sum(t):
+        to_all(lambda to: drain(gunits.at[0], 8))
+        at_peers(0, ndp, lambda c, to: drain(gcoded.at[t, c], 7))
+        across(t, lambda c, to: drain(gcoded.at[t, c], 9))
 
     @pl.when(owner)
     def _():
-        loop(ndev - 1, lambda k: drain(sums.at[slot], 1))
-        loop(ndev - 1, lambda k: drain(gunits.at[slot], 8))
-        gathers(
-            lambda c, to: drain(gcoded.at[c], 7),
-            lambda t, c, to: drain(gcoded.at[c, t], 9),
-        )
+        to_all(lambda to: drain(sums.at[slot], 1))
+        drain_sum(0)
+
+        @pl.when(extra)
+        def _():
+            drain_sum(1)
 
     pltpu.make_async_copy(others, others, send_sem.at[2]).wait()
     pltpu.make_async_copy(others, others, send_sem.at[3]).wait()
@@ -635,19 +717,19 @@
             pltpu.VMEM((1, rows), F32),
             pltpu.VMEM((1, 1), jnp.int32),
             pltpu.VMEM((parts, ndp * rows * SUB, LANES), F32),
-            pltpu.VMEM((parts, ndp // 2, 2 * rows * SUB, LANES), I16),
-            pltpu.VMEM((ndp // 2, parts, LANES), F32),
-            pltpu.VMEM((2 * ndp, 2 * height, LANES), I16),
-            pltpu.VMEM((2 * ndp, parts, LANES), F32),
+            pltpu.VMEM((parts, ndp, rows * SUB, LANES), I16),
+            pltpu.VMEM((ndp, parts, LANES), F32),
+            pltpu.VMEM((2, 2 * ndp, *block), I16),
+            pltpu.VMEM((2, 2 * ndp, parts, LANES), F32),
             pltpu.VMEM((ndp // 2, 2, 3 * height, LANES), I16),
             pltpu.VMEM((ndp, 2, LANES), F32),
             pltpu.VMEM((nmp, 2 * height, LANES), I16),
             pltpu.VMEM((nmp, 2 * parts * SUB, LANES), F32),
-            pltpu.VMEM((ndp // 2, 2, *block), I16),
+            pltpu.VMEM((ndp, *block), I16),
             pltpu.VMEM((nmp, *block), I16),
-            pltpu.VMEM((ndp * nmp // 4, 2, LANES), F32),
-            pltpu.VMEM((ndp * nmp // 4, 1, LANES), F32),
-            pltpu.VMEM((2, 2 * height, LANES), F32),
+            pltpu.VMEM((nmp // 2 * ndp, 2, LANES), F32),
+            pltpu.VMEM((nmp // 2 * (ndp - ndp // 4), 1, LANES), F32),
+            pltpu.VMEM((2, 2, *block), F32),
             pltpu.VMEM((2, 2, *block), I16),
             pltpu.VMEM(block, F32),
             pltpu.VMEM(block, F32),
@@ -659,7 +741,9 @@
             pltpu.VMEM((nmp, *block), F32),
             pltpu.SemaphoreType.DMA((9,)),
             pltpu.SemaphoreType.DMA((parts * loads,)),
+            pltpu.SemaphoreType.REGULAR((2,)),
             pltpu.SemaphoreType.DMA((ndp // 2,)),
+            pltpu.SemaphoreType.DMA((4,)),
             pltpu.SemaphoreType.DMA((13,)),
             pltpu.SemaphoreType.DMA((13,)),
         ],

time: 19.8 us -> 19.3 us (0.975)
  the two profiles are of different devices: /device:TPU:0 before, /device:TPU:1 now
where the time goes in v1:
time: 19.3 us; the launch traced here: 19.1 us
  Pallas kernels  17.8 us (92%)
  between operations  1.3 us (7%)
    pallas_call x1, Pallas kernels, shards(): pl.pallas_call(functools.partial(kernel, ndp, nmp, loads), out_shape=(den...  17.1 us
    pallas_call x1, Pallas kernels, shards(): pl.pallas_call(unpack, out_shape=(whole, whole, jax.ShapeDtypeStruct((ndp...  0.76 us

profile of v1, /device:TPU:1, one launch (start us, length us, event | category | flops | bytes accessed | tf_op | source)
XLA Modules:
  0.0 19.1 jit_solution(5129323853622863297)
XLA Ops:
  1.3 17.1 %shard_map.169 = (f32[48,128]{1,0:T(8,128)S(1)}, f32[48,128]{1,0:T(8,128)S(1)}, bf16[8,48,128]{2,1,0:T(8,128)(2,1)S(1)}, f32[48,128]{1,0:T(8,128)S(1)}, f32[48,1...) custom-call(bf16[24,1024]{1,0:T(8,128)(2,1)} %bitcast.9, bf16[1024,2048]{1,0:T(8,128)(2,1)} %cot_hbm.1, ...), custom_call_target="tpu_custom_call" | custom-call | tf_op jit(solution)/shard_map/pallas_call | solution.py:697
  18.4 0.8 %shard_map.170 = (f32[3,2048]{1,0:T(4,128)}, f32[3,2048]{1,0:T(4,128)}, bf16[24,2048]{1,0:T(8,128)(2,1)}, f32[3,2048]{1,0:T(4,128)}, f32[3,2048]{1,0:T(4,128)}, ...) custom-call(f32[48,128]{1,0:T(8,128)S(1)} %get-tuple-element.25.master, ...), custom_call_target="tpu_custom_call" | custom-call | tf_op jit(solution)/shard_map/pallas_call | solution.py:767

commit v2 on v1

--- a/solution.py
+++ b/solution.py
@@ -387,6 +387,17 @@
 
         loop(ndev, step)
 
+    def to_readers(t, body):
+        row = later if t else dp
+
+        def other(to):
+            @pl.when(lax.div(to, 2) != group)
+            def _():
+                body({"dp": row, "mp": to})
+
+        at_peers(0, ndp, lambda c, to: body(to))
+        loop(nmp, other)
+
     def collect(t):
         j = later if t else dp
         for p in range(parts):
@@ -421,35 +432,20 @@
             gcoded[t, c] = coded
         gq[j] = gcoded[t, 1]
 
-    def send_sum(t):
+    def send_near(t):
         j = later if t else dp
         units = gunits.at[group * ndp + j]
-        to_all(lambda to: send(units, units, 8, to))
+        to_readers(t, lambda to: send(units, units, 8, to))
         at_peers(0, quarter, lambda c, to: send(gcoded.at[t, c], gq.at[j], 7, to))
+
+    def send_far(t):
+        j = later if t else dp
         across(t, lambda c, to: send(gcoded.at[t, c], gm.at[2 * group + c], 9, to))
         at_peers(
             quarter,
             ndp - quarter,
             lambda c, to: send(gcoded.at[t, c], gq.at[j], 7, to),
         )
-
-    @pl.when(owner)
-    def _():
-        sums[slot] = collect(0)
-
-        @pl.when(extra)
-        def _():
-            sums[slot] = sums[slot] + collect(1)
-
-        to_all(lambda to: send(sums.at[slot], sums.at[slot], 1, to))
-        code_sum(0)
-        gm[mp - 1] = gcoded[0, 0]
-        send_sum(0)
-
-        @pl.when(extra)
-        def _():
-            code_sum(1)
-            send_sum(1)
 
     column = packs.at[:, side]
     others = column.at[pl.ds(0, ndp // 2 - 1)]
@@ -465,7 +461,38 @@
 
         loop(ndp // 2 - 1, forward)
 
-    relay()
+    @pl.when(half == 0)
+    def _():
+        relay()
+
+    @pl.when(owner)
+    def _():
+        sums[slot] = collect(0)
+
+        @pl.when(extra)
+        def _():
+            sums[slot] = sums[slot] + collect(1)
+
+        to_all(lambda to: send(sums.at[slot], sums.at[slot], 1, to))
+        code_sum(0)
+        gm[mp - 1] = gcoded[0, 0]
+
+        @pl.when(extra)
+        def _():
+            code_sum(1)
+            send_near(1)
+
+        send_near(0)
+        send_far(0)
+
+        @pl.when(extra)
+        def _():
+            send_far(1)
+
+    @pl.when(half > 0)
+    def _():
+        relay()
+
     wait_all(metas, ndp - 1, recv_sem.at[4])
     wait_all(mcodes, nmp - 1, recv_sem.at[5])
     wait_all(mcols, nmp - 1, recv_sem.at[6])
@@ -538,7 +565,7 @@
         change = number(code) * (unit * clipf)
         return m1 + 0.1 * change, m2 + 0.05 * (change * change)
 
-    settle(gunits, nmp // 2 * ndp, 8, 2)
+    settle(gunits, ndp + nmp // 2 - 1, 8, 2)
     settle(gq, ndp, 7, 2)
     settle(gm, nmp - 1, 9, 1)
     gm[mp] = gq[dp]
@@ -601,7 +628,7 @@
     to_owners(lambda j, t, to: drain(share_unit.at[j], 11))
 
     def drain_sum(t):
-        to_all(lambda to: drain(gunits.at[0], 8))
+        to_readers(t, lambda to: drain(gunits.at[0], 8))
         at_peers(0, ndp, lambda c, to: drain(gcoded.at[t, c], 7))
         across(t, lambda c, to: drain(gcoded.at[t, c], 9))
 
@@ -685,7 +712,7 @@
     rows, ncols = master_weights.shape
     tokens, width = hidden_input.shape
     parts = ncols // (SUB * LANES)
-    loads = 2
+    loads = 4
     height = parts * rows * SUB
     hbm = pl.BlockSpec(memory_space=pltpu.HBM)
     smem = pl.BlockSpec(memory_space=pltpu.SMEM)

time: 19.3 us -> 18.7 us (0.969)
  the two profiles are of different devices: /device:TPU:1 before, /device:TPU:0 now
where the time goes in v2:
time: 18.7 us; the launch traced here: 18.4 us
  Pallas kernels  17.1 us (91%)
  between operations  1.3 us (7%)
    pallas_call x1, Pallas kernels, shards(): pl.pallas_call(functools.partial(kernel, ndp, nmp, loads), out_shape=(den...  16.3 us
    pallas_call x1, Pallas kernels, shards(): pl.pallas_call(unpack, out_shape=(whole, whole, jax.ShapeDtypeStruct((ndp...  0.76 us

profile of v2, /device:TPU:0, one launch (start us, length us, event | category | flops | bytes accessed | tf_op | source)
XLA Modules:
  0.0 18.4 jit_solution(4084394083969406758)
XLA Ops:
  1.3 16.3 %shard_map.169 = (f32[48,128]{1,0:T(8,128)S(1)}, f32[48,128]{1,0:T(8,128)S(1)}, bf16[8,48,128]{2,1,0:T(8,128)(2,1)S(1)}, f32[48,128]{1,0:T(8,128)S(1)}, f32[48,1...) custom-call(bf16[24,1024]{1,0:T(8,128)(2,1)} %bitcast.9, bf16[1024,2048]{1,0:T(8,128)(2,1)} %cot_hbm.1, ...), custom_call_target="tpu_custom_call" | custom-call | tf_op jit(solution)/shard_map/pallas_call | solution.py:724
  17.6 0.8 %shard_map.170 = (f32[3,2048]{1,0:T(4,128)}, f32[3,2048]{1,0:T(4,128)}, bf16[24,2048]{1,0:T(8,128)(2,1)}, f32[3,2048]{1,0:T(4,128)}, f32[3,2048]{1,0:T(4,128)}, ...) custom-call(f32[48,128]{1,0:T(8,128)S(1)} %get-tuple-element.25.master, ...), custom_call_target="tpu_custom_call" | custom-call | tf_op jit(solution)/shard_map/pallas_call | solution.py:794

commit v3 on v2

--- a/solution.py
+++ b/solution.py
@@ -712,7 +712,7 @@
     rows, ncols = master_weights.shape
     tokens, width = hidden_input.shape
     parts = ncols // (SUB * LANES)
-    loads = 4
+    loads = 2
     height = parts * rows * SUB
     hbm = pl.BlockSpec(memory_space=pltpu.HBM)
     smem = pl.BlockSpec(memory_space=pltpu.SMEM)

time: 18.7 us -> 18.5 us (0.989)
  Pallas kernels: 17.1 us -> 16.9 us
where the time goes in v3:
time: 18.5 us; the launch traced here: 18.2 us
  Pallas kernels  16.9 us (91%)
  between operations  1.3 us (7%)
    pallas_call x1, Pallas kernels, shards(): pl.pallas_call(functools.partial(kernel, ndp, nmp, loads), out_shape=(den...  16.1 us
    pallas_call x1, Pallas kernels, shards(): pl.pallas_call(unpack, out_shape=(whole, whole, jax.ShapeDtypeStruct((ndp...  0.76 us

profile of v3, /device:TPU:0, one launch (start us, length us, event | category | flops | bytes accessed | tf_op | source)
XLA Modules:
  0.0 18.2 jit_solution(1941595937679703724)
XLA Ops:
  1.3 16.1 %shard_map.169 = (f32[48,128]{1,0:T(8,128)S(1)}, f32[48,128]{1,0:T(8,128)S(1)}, bf16[8,48,128]{2,1,0:T(8,128)(2,1)S(1)}, f32[48,128]{1,0:T(8,128)S(1)}, f32[48,1...) custom-call(bf16[24,1024]{1,0:T(8,128)(2,1)} %bitcast.9, bf16[1024,2048]{1,0:T(8,128)(2,1)} %cot_hbm.1, ...), custom_call_target="tpu_custom_call" | custom-call | tf_op jit(solution)/shard_map/pallas_call | solution.py:724
  17.4 0.8 %shard_map.170 = (f32[3,2048]{1,0:T(4,128)}, f32[3,2048]{1,0:T(4,128)}, bf16[24,2048]{1,0:T(8,128)(2,1)}, f32[3,2048]{1,0:T(4,128)}, f32[3,2048]{1,0:T(4,128)}, ...) custom-call(f32[48,128]{1,0:T(8,128)S(1)} %get-tuple-element.25.master, ...), custom_call_target="tpu_custom_call" | custom-call | tf_op jit(solution)/shard_map/pallas_call | solution.py:794
